TPU v7x, 32 devices: a whole 2x2x4 slice. The times are simulated.
32 devices in a mesh: groups: 2 (over x), rows: 16 (over z, y, core).
Axes of the slice: x: 2, y: 2, z: 4, core: 2. Of those that a mesh axis runs over, the one named last changes fastest.
Arguments:
- frames: bfloat16 [16384, 2560], P(('groups', 'rows')), parts along dimension 0, may hold values from -6 to 6
- offsets: int32 [4096], P(('groups', 'rows')), parts along dimension 0, may hold values from 0 to 8173, as said below
- neighbours: int32 [32, 4096], P(None, ('groups', 'rows')), parts along dimension 1, may hold values from 0 to 2047, as said below
- initial_codes: int32 [32, 4096], P(None, ('groups', 'rows')), parts along dimension 1, may hold values from -1048576 to 1048575
- embed_weight: bfloat16 [2560, 256], replicated, may hold values from -0.125 to 0.125
- embed_bias: float32 [256], replicated, may hold values from -0.9 to 0.9
Outputs:
- affinity: float32 [32, 4096], P(None, ('groups', 'rows')), parts along dimension 1
- vectors: float32 [32, 4096], P(None, ('groups', 'rows')), parts along dimension 1
There are 2 independent parts, one for each index of `groups`. A program takes and returns all parts, laid end to end along the dimension named above; an argument that names none is the same for every part. Nothing has to cross between parts.
Inputs may be any that keep to these rules, and one draw needn't show every extreme that they name: `offsets`: the window of row i starts in the block of 512 frames numbered i // 128 and its 19 frames end before frame 8192. `neighbours`: the 32 columns of row i are distinct and differ from i; the k-th is (i + d) mod 2048 with 1 + k s <= d <= (k + 1) s, where s = 63.
All inputs are finite; a program needn't handle non-finite values.
Results may differ from a plain program's by a relative error of at most 0.012.
The roundings to bfloat16 on the way count: a program that leaves them out, or rounds other values in their place, can miss the bound.
Values may be sent and summed in bfloat16 or wider, within the bound.
A program may use at most 64 MiB of HBM per device.

v0:
```python
import jax
import jax.numpy as jnp
from jax import lax
from jax.sharding import PartitionSpec as P

WIN = 19
ITERS = 3


epsilon = 1e-06
sharpness = 8.0
seed_scale = 2.0 ** (-20)


def from_behind(block, axis, distance):
    devices = range(lax.axis_size(axis))
    route = [(i - distance, i) for i in devices if i - distance in devices]
    return lax.ppermute(block, axis, route)


def block_width(length, shard_rows):
    shards = length // shard_rows
    chosen = 1
    for factor in range(1, shards + 1):
        if shards % factor == 0 and factor * shard_rows <= 4096:
            chosen = factor
    return chosen * shard_rows


def on_device(frames, offsets, neighbours, initial_codes, embed_weight, embed_bias):
    own_rows = offsets.shape[0]
    own_frames = frames.shape[0]
    kept = neighbours.shape[0]
    my_index = lax.axis_index("rows")
    next_frames = from_behind(frames[: WIN - 1], "rows", -1)
    extended = jnp.concatenate([frames, next_frames], axis=0)
    window_start = offsets - my_index * own_frames
    positions = jnp.arange(extended.shape[0], dtype=jnp.int32)[None, :]
    begins = window_start[:, None]
    window_mask = ((positions >= begins) & (positions < begins + WIN)).astype(jnp.bfloat16)
    window_sums = jnp.dot(window_mask, extended, preferred_element_type=jnp.float32)
    pooled = (window_sums * (1.0 / WIN)).astype(jnp.bfloat16)
    embedded = jnp.dot(pooled, embed_weight, preferred_element_type=jnp.float32) + embed_bias
    squares = jnp.sum(embedded * embedded, axis=1, keepdims=True)
    unit_rows = (embedded * lax.rsqrt(squares + epsilon)).astype(jnp.bfloat16)
    portion = lax.all_gather(unit_rows, "rows", axis=0, tiled=True)
    length = portion.shape[0]
    block_cols = block_width(length, own_rows)

    def one_block(block_index, carried):
        first_col = block_index * block_cols
        candidates = lax.dynamic_slice_in_dim(portion, first_col, block_cols, 0)
        scores = lax.dot_general(
            unit_rows, candidates, (((1,), (1,)), ((), ())), preferred_element_type=jnp.float32
        )
        relative = neighbours - first_col
        inside = (relative >= 0) & (relative < block_cols)
        picked = jnp.take_along_axis(scores, jnp.clip(relative, 0, block_cols - 1).T, axis=1).T
        return carried + jnp.where(inside, picked, 0.0)

    cosine = lax.fori_loop(
        0, length // block_cols, one_block, jnp.zeros((kept, own_rows), jnp.float32)
    )
    affinity = jnp.exp(sharpness * (cosine - 1.0))
    vectors = initial_codes.astype(jnp.float32) * seed_scale
    vec_count = vectors.shape[0]
    carried = vectors
    for turn_index in range(ITERS):
        gathered = lax.all_gather(carried, "rows", axis=1, tiled=True)
        if turn_index > 0:
            gram_matrix = jnp.dot(gathered, gathered.T, precision=lax.Precision.HIGHEST)
            cholesky_factor = jnp.linalg.cholesky(gram_matrix)
            gathered = jax.scipy.linalg.solve_triangular(cholesky_factor, gathered, lower=True)
        current = lax.dynamic_slice_in_dim(gathered, my_index * own_rows, own_rows, 1)
        forward = jnp.sum(affinity[None] * jnp.take(gathered, neighbours, axis=1), axis=1)
        spread = (
            jnp.zeros((vec_count, gathered.shape[1]), jnp.float32)
            .at[:, neighbours.reshape(-1)]
            .add((affinity[None] * current[:, None, :]).reshape(vec_count, -1))
        )
        mixed = 0.5 * (forward + lax.psum_scatter(spread, "rows", scatter_dimension=1, tiled=True))
        carried = mixed
    partial_gram = jnp.dot(carried, carried.T, precision=lax.Precision.HIGHEST)
    gram_matrix = lax.psum(partial_gram, "rows")
    cholesky_factor = jnp.linalg.cholesky(gram_matrix)
    carried = jax.scipy.linalg.solve_triangular(cholesky_factor, carried, lower=True)
    return (affinity, carried)


def solution(mesh):
    placed = (
        P(("groups", "rows"), None),
        P(("groups", "rows")),
        P(None, ("groups", "rows")),
        P(None, ("groups", "rows")),
        P(),
        P(),
    )
    return jax.shard_map(
        on_device,
        mesh=mesh,
        in_specs=placed,
        out_specs=(P(None, ("groups", "rows")), P(None, ("groups", "rows"))),
        check_vma=False,
    )
```

profile of v0, /device:TPU:0, one launch (start us, length us, event | category | flops | bytes accessed | tf_op | source)
XLA Modules:
  0.0 474.0 jit_solution(6266484893465082726)
XLA Ops:
  8.2 1.3 collective-permute-start
  11.5 2.9 multiply_reduce_fusion
  15.4 25.2 %all_gather.13 = f32[32,2048]{1,0:T(8,128)S(1)} all-gather(f32[32,128]{1,0:T(8,128)S(1)} %convert_multiply_fusion), channel_id=1, replica_groups=mesh['groups'=2,'rows'=16] {'rows'}, dimensions={1}, use_global_device_ids=true | all-gather | bytes 278528 | tf_op jit(solution)/shard_map/all_gather | solution.py:69
  41.1 14.1 %gather_fusion.1 = f32[4096,32]{1,0:T(8,128)} fusion(f32[32,2048]{0,1:T(8,128)S(1)} %copy.50, s32[4096]{0:T(1024)S(1)} %bitcast_clamp_fusion), kind=kCustom, calls=%fused_computation.clone | custom fusion | bytes 1064960 | tf_op jit(solution)/shard_map/jit(_take)/gather | solution.py:75
  55.2 3.1 all-gather.2.cloned.1.call-done
  58.3 1.7 fusion.64
  60.0 32.8 %gather_fusion = f32[4096]{0:T(1024)S(1)} fusion(f32[128,2048]{1,0:T(8,128)S(1)} %fusion.64, s32[4096]{0:T(1024)S(1)} %reshape.113), kind=kCustom, calls=%fused_computation.3 | custom fusion | bytes 65536 | tf_op jit(solution)/shard_map/while/body/eval_jaxpr/jit(take_along_axis)/gather | solution.py:58
  93.6 23.4 %scatter_custom_fusion = f32[32,2048]{0,1:T(8,128)} fusion(s32[4096]{0:T(1024)S(1)} %bitcast.98, f32[32,4096]{0,1:T(8,128)S(1)} %bitcast_multiply_fusion.4, f32[]{:T(128)} %constant.102.clone.1), kind=kCustom, calls=%fused_computation.22 | custom fusion | flops 131072 | bytes 2359300 | tf_op jit(solution)/shard_map/scatter-add | solution.py:79
  117.1 3.2 fusion.12
  120.3 53.4 %reduce-scatter.4.cloned.1.call-done = f32[32,128]{0,1:T(8,128)} async-done(((f32[32,2048]{0,1:T(8,128)}), f32[32,128]{0,1:T(8,128)}) %reduce-scatter.4.cloned.1.call-update) | async-done | bytes 16400 | tf_op jit(solution)/shard_map/reduce_scatter | solution.py:81
  174.6 22.6 %all_gather.14 = f32[32,2048]{0,1:T(8,128)S(1)} all-gather(f32[32,128]{0,1:T(8,128)S(1)} %add_multiply_fusion.2), channel_id=1, replica_groups=mesh['groups'=2,'rows'=16] {'rows'}, dimensions={1}, use_global_device_ids=true | all-gather | bytes 278528 | tf_op jit(solution)/shard_map/all_gather | solution.py:69
  197.1 1.8 fusion.65
  199.0 2.9 cholesky.59
  203.3 2.4 custom-call.13
  208.4 23.4 %scatter_custom_fusion.1 = f32[32,2048]{0,1:T(8,128)} fusion(s32[4096]{0:T(1024)S(1)} %bitcast.99, f32[32,4096]{0,1:T(8,128)S(1)} %bitcast_multiply_fusion.2, f32[]{:T(128)} %constant.102.clone.1), kind=kCustom, calls=%fused_computation.17 | custom fusion | flops 131072 | bytes 2359300 | tf_op jit(solution)/shard_map/scatter-add | solution.py:79
  232.0 1.3 copy.54
  233.3 14.1 %gather_fusion.2 = f32[4096,32]{1,0:T(8,128)} fusion(f32[32,2048]{0,1:T(8,128)S(1)} %copy.54, s32[4096]{0:T(1024)S(1)} %bitcast_clamp_fusion), kind=kCustom, calls=%fused_computation.1.clone | custom fusion | bytes 1064960 | tf_op jit(solution)/shard_map/jit(_take)/gather | solution.py:75
  247.4 3.2 fusion.9
  250.6 36.3 %reduce-scatter.6.cloned.1.call-done = f32[32,128]{0,1:T(8,128)} async-done(((f32[32,2048]{0,1:T(8,128)}), f32[32,128]{0,1:T(8,128)}) %reduce-scatter.6.cloned.1.call-update) | async-done | bytes 16400 | tf_op jit(solution)/shard_map/reduce_scatter | solution.py:81
  287.8 22.6 %all_gather.15 = f32[32,2048]{0,1:T(8,128)S(1)} all-gather(f32[32,128]{0,1:T(8,128)S(1)} %add_multiply_fusion.1), channel_id=1, replica_groups=mesh['groups'=2,'rows'=16] {'rows'}, dimensions={1}, use_global_device_ids=true | all-gather | bytes 278528 | tf_op jit(solution)/shard_map/all_gather | solution.py:69
  310.3 1.8 fusion.66
  312.2 2.9 cholesky.70
  316.5 2.4 custom-call.14
  321.6 23.4 %scatter_custom_fusion.2 = f32[32,2048]{0,1:T(8,128)} fusion(s32[4096]{0:T(1024)S(1)} %bitcast.100, f32[32,4096]{0,1:T(8,128)S(1)} %bitcast_multiply_fusion, f32[]{:T(128)} %constant.102.clone.1), kind=kCustom, calls=%fused_computation.12 | custom fusion | flops 131072 | bytes 2359300 | tf_op jit(solution)/shard_map/scatter-add | solution.py:79
  345.0 1.3 copy.57
  346.3 14.1 %gather_fusion.3 = f32[4096,32]{1,0:T(8,128)} fusion(f32[32,2048]{0,1:T(8,128)S(1)} %copy.57, s32[4096]{0:T(1024)S(1)} %bitcast_clamp_fusion), kind=kCustom, calls=%fused_computation.2.clone | custom fusion | bytes 1064960 | tf_op jit(solution)/shard_map/jit(_take)/gather | solution.py:75
  360.4 3.2 fusion.6
  363.6 36.6 %reduce-scatter.8.cloned.1.call-done = f32[32,128]{0,1:T(8,128)} async-done(((f32[32,2048]{0,1:T(8,128)}), f32[32,128]{0,1:T(8,128)}) %reduce-scatter.8.cloned.1.call-update) | async-done | bytes 16400 | tf_op jit(solution)/shard_map/reduce_scatter | solution.py:81
  401.3 57.6 %psum.7 = f32[32,32]{0,1:T(8,128)S(1)} all-reduce(f32[32,32]{0,1:T(8,128)S(1)} %fusion.39), channel_id=1, replica_groups=mesh['groups'=2,'rows'=16] {'rows'}, use_global_device_ids=true, to_apply=%region_12.16 | all-reduce | flops 1024 | bytes 8192 | tf_op jit(solution)/shard_map/psum | solution.py:84
  459.0 2.9 cholesky.81
  463.3 2.4 custom-call.9
  465.7 1.7 fusion.38
  (67 shorter events, 17.9 us)
Async XLA Ops:
  7.2 4.3 copy-start
  7.2 51.1 %all-gather.2.cloned.1.call-start = ((), (), s32[]{:S(2)}) async-start(), calls=%async_computation.3 | async-start | bytes 1114112 | tf_op jit(solution)/shard_map/all_gather | solution.py:46
  8.2 3.2 collective-permute-start
  11.5 3.7 copy-start.5
  11.5 3.9 copy-start.6
  15.1 158.6 %reduce-scatter.4.cloned.1.call-start = ((), (), s32[]{:S(2)}) async-start(), calls=%async_computation.4 | async-start | bytes 1114112 | tf_op jit(solution)/shard_map/reduce_scatter | solution.py:81
  41.0 17.3 %copy-start.4 = (bf16[128,256]{1,0:T(8,128)(2,1)S(1)}, bf16[128,256]{1,0:T(8,128)(2,1)}, u32[]{:S(2)}) copy-start(bf16[128,256]{1,0:T(8,128)(2,1)} %multiply_convert_fusion) | copy-start | bytes 196612
  93.0 267.4 %copy-start.3 = (f32[32,128]{1,0:T(8,128)}, f32[32,128]{1,0:T(8,128)S(1)}, u32[]{:S(2)}) copy-start(f32[32,128]{1,0:T(8,128)S(1)} %copy.61) | copy-start | bytes 49156
  117.0 169.9 %reduce-scatter.6.cloned.1.call-start = ((), (), s32[]{:S(2)}) async-start(), calls=%async_computation.5 | async-start | bytes 1114112 | tf_op jit(solution)/shard_map/reduce_scatter | solution.py:81
  206.9 0.7 copy-start.2
  231.8 168.4 %reduce-scatter.8.cloned.1.call-start = ((), (), s32[]{:S(2)}) async-start(), calls=%async_computation.6 | async-start | bytes 1114112 | tf_op jit(solution)/shard_map/reduce_scatter | solution.py:81
  320.2 0.7 copy-start.1
Sparse Core Ops, SparseCore 0:
  15.2 43.0 all-gather.1
  117.1 56.5 reduce-scatter.3
  231.9 54.9 reduce-scatter.5
  345.1 55.0 reduce-scatter.7
where the time goes:
time: 475 us; the launch traced here: 474 us
  waiting for transfers between devices  131 us (28%)
  blocking collectives  128 us (27%)
  other arithmetic  105 us (22%)
  local copies, waits for them, and re-layouts  81.2 us (17%)
  between operations  14 us (3%)
  matrix products  13.5 us (3%)
    reduce_scatter x3, waiting for transfers between devices, on_device(): lax.psum_scatter(spread, 'rows', scatter_dimension=1, tiled=True)  126 us
    all_gather x3, blocking collectives, on_device(): gathered = lax.all_gather(carried, 'rows', axis=1, tiled=True)  70.3 us
    scatter-add x3, other arithmetic, on_device(): spread = jnp.zeros((vec_count, gathered.shape[1]), jnp.float32).at[:, nei...  70.2 us
    psum x1, blocking collectives, on_device(): gram_matrix = lax.psum(partial_gram, 'rows')  57.6 us
    gather x3, local copies, waits for them, and re-layouts, on_device(): jnp.take(gathered, neighbours, axis=1)  42.3 us
    gather x3, local copies, waits for them, and re-layouts, one_block(): jnp.take_along_axis(scores, jnp.clip(relative, 0, block_cols - 1).T, axis=1)  32.9 us
    another operation x9, other arithmetic, on_device(): cholesky_factor = jnp.linalg.cholesky(gram_matrix)  10.8 us
    reduce_sum x3, other arithmetic, on_device(): jnp.sum(affinity[None] * jnp.take(gathered, neighbours, axis=1), axis=1)  9.57 us
  transfers between devices with their start and end apart: 5, of which 5 were waited for; matrix products, arithmetic and copies ran while one was open for 12% of the time, Pallas kernels for 0%

commit v1 on v0

v1 whole, which is shorter than its diff:
```python
import functools

import jax
import jax.numpy as jnp
from jax import lax
from jax.experimental import pallas as pl
from jax.experimental.pallas import tpu as pltpu
from jax.sharding import PartitionSpec as P

WIN = 19
ITERS = 3
HALO = 32

epsilon = 1e-06
sharpness = 8.0
seed_scale = 2.0 ** (-20)
HIGH = lax.Precision.HIGHEST


def bands(block, count, rows, kept):
    total = count * rows
    stride = (total - 1) // kept
    found = set()
    for delta in range(1 - rows, rows):
        distance = (rows * block + delta) % total
        if distance >= 1 and (distance - 1) // stride < kept:
            found.add((distance - 1) // stride)
    return sorted(found)


def split(value):
    high = value.astype(jnp.bfloat16)
    low = (value - high.astype(jnp.float32)).astype(jnp.bfloat16)
    return high, low


def inverse_factor(gram):
    size = gram.shape[0]
    row = lax.broadcasted_iota(jnp.int32, (size, size), 0)
    lane = lax.broadcasted_iota(jnp.int32, (size, size), 1)
    eye = jnp.where(row == lane, 1.0, 0.0).astype(jnp.float32)
    work = jnp.concatenate([gram, eye], axis=1)
    tall = lax.broadcasted_iota(jnp.int32, (size, 1), 0)
    for j in range(size):
        pivot_row = work[j : j + 1, :]
        factor = work[:, j : j + 1] * (1.0 / work[j : j + 1, j : j + 1])
        work = work - jnp.where(tall > j, factor, 0.0) * pivot_row
    diagonal = jnp.sum(jnp.where(row == lane, work[:, :size], 0.0), axis=1, keepdims=True)
    return work[:, size:] * lax.rsqrt(diagonal)


def kernel(
    n, frames, weight, offsets, neighbours, codes, bias, affinity, vectors,
    frames_v, weight_v, halo, sums, units, starts, masks, s_high, s_low, mixes, grams,
    load_sem, halo_sem, send_sem, recv_sem, hop_sem,
):
    own_frames, channels = frames.shape
    kept, rows = neighbours.shape
    vec = codes.shape[0]
    total = n * rows
    me = lax.axis_index("rows")
    odd = lax.rem(me, 2)
    sibling = me + 1 - 2 * odd
    shift = 2 * odd - 1
    chunk = 512 if channels % 512 == 0 else 128
    chunks = channels // chunk

    loads = []
    for c in range(chunks):
        cut = pl.ds(c * chunk, chunk)
        loads.append(pltpu.make_async_copy(frames.at[:, cut], frames_v.at[:, cut], load_sem.at[c]))
    weight_load = pltpu.make_async_copy(weight, weight_v, load_sem.at[chunks])
    for load in loads:
        load.start()
    weight_load.start()

    barrier = pltpu.get_barrier_semaphore()
    for ahead in range(1, n):
        pl.semaphore_signal(barrier, inc=1, device_id={"rows": lax.rem(me + ahead, n)})

    starts[0, :vec, :] = codes[...].astype(jnp.float32) * seed_scale
    first = me * rows
    relative = neighbours[...] - first
    relative = jnp.where(relative < 0, relative + total, relative).astype(jnp.float32)
    starts[0, vec:, :] = relative

    pl.semaphore_wait(barrier, n - 1)

    sent = []

    def remote(src, dst, a, b, target):
        return pltpu.make_async_remote_copy(
            src_ref=src, dst_ref=dst, send_sem=a, recv_sem=b, device_id={"rows": target}
        )

    def launch(buffer, phase):
        order = []
        for c in range(1, n // 4 + 1):
            order.append(2 * c)
            if n - 2 * c != 2 * c:
                order.append(n - 2 * c)
        order = sorted(set(e for e in order if 0 < e < n))
        order = sorted(order, key=lambda e: -min(e, n - e))
        near = remote(
            buffer.at[0], buffer.at[lax.rem(shift + n, n)], hop_sem.at[phase, 0],
            recv_sem.at[phase, lax.rem(shift + n, n)], sibling,
        )
        near.start()
        sent.append(near)
        for e in order:
            copy = remote(
                buffer.at[0], buffer.at[n - e], send_sem.at[phase, e],
                recv_sem.at[phase, n - e], lax.rem(me + e, n),
            )
            copy.start()
            sent.append(copy)

    def arrived(buffer, phase, r):
        remote(
            buffer.at[0], buffer.at[r], send_sem.at[phase, r], recv_sem.at[phase, r], sibling
        ).wait_recv()

    def forward_on(buffer, phase, e):
        slot = lax.rem(e + shift + n, n)
        copy = remote(
            buffer.at[e], buffer.at[slot], hop_sem.at[phase, e], recv_sem.at[phase, slot], sibling
        )
        copy.start()
        sent.append(copy)

    arrival_order = sorted(range(2, n, 2), key=lambda e: min(e, n - e))

    behind = lax.rem(me + n - 1, n)
    halo_copy = remote(
        frames.at[pl.ds(0, HALO), :], halo, halo_sem.at[0], halo_sem.at[1], behind
    )
    halo_copy.start()
    launch(starts, 0)

    begins = offsets[...] - me * own_frames
    begins = jnp.transpose(jnp.broadcast_to(begins, (rows, rows)))
    column = lax.broadcasted_iota(jnp.int32, (rows, rows), 1)

    def window(base, width):
        pieces = []
        for at in range(0, width, rows):
            size = min(rows, width - at)
            position = (column + (base + at))[:, :size]
            start = begins[:, :size]
            inside = (position >= start) & (position < start + WIN)
            pieces.append(jnp.where(inside, 1.0, 0.0).astype(jnp.bfloat16))
        return jnp.concatenate(pieces, axis=1) if len(pieces) > 1 else pieces[0]

    body_mask = window(0, own_frames)
    rim_mask = window(own_frames, HALO)
    for c in range(chunks):
        cut = pl.ds(c * chunk, chunk)
        loads[c].wait()
        sums[:, cut] = jnp.dot(body_mask, frames_v[:, cut], preferred_element_type=jnp.float32)
    weight_load.wait()
    halo_copy.wait_recv()
    embedded = jnp.zeros((rows, weight.shape[1]), jnp.float32)
    for c in range(chunks):
        cut = pl.ds(c * chunk, chunk)
        whole = sums[:, cut] + jnp.dot(rim_mask, halo[:, cut], preferred_element_type=jnp.float32)
        pooled = (whole * (1.0 / WIN)).astype(jnp.bfloat16)
        embedded = embedded + jnp.dot(pooled, weight_v[cut, :], preferred_element_type=jnp.float32)
    embedded = embedded + bias[...]
    squares = jnp.sum(embedded * embedded, axis=1, keepdims=True)
    units[0] = (embedded * lax.rsqrt(squares + epsilon)).astype(jnp.bfloat16)
    launch(units, 1)

    for e in arrival_order:
        arrived(starts, 0, e)
        forward_on(starts, 0, e)
    down = lax.broadcasted_iota(jnp.int32, (rows, rows), 0).astype(jnp.float32)
    for r in [0] + arrival_order + list(range(1, n, 2)):
        if r % 2 == 1:
            arrived(starts, 0, r)
        mine = jnp.zeros((rows, rows), jnp.float32)
        for k in bands(r, n, rows, kept):
            mine = jnp.where(down == starts[0, vec + k : vec + k + 1, :] - rows * r, 0.5, mine)
        back = (n - r) % n
        theirs = jnp.zeros((rows, rows), jnp.float32)
        for k in bands(back, n, rows, kept):
            theirs = jnp.where(down == starts[r, vec + k : vec + k + 1, :] - rows * back, 0.5, theirs)
        masks[r] = mine + jnp.transpose(theirs)

    affinity[...] = jnp.zeros_like(affinity)
    mine_units = units[0]

    def score(r):
        scores = lax.dot_general(
            units[r], mine_units, (((1,), (1,)), ((), ())), preferred_element_type=jnp.float32
        )
        dense = jnp.exp(sharpness * (scores - 1.0))
        high, low = split(dense * masks[r])
        s_high[pl.ds(r * rows, rows), :] = high
        s_low[pl.ds(r * rows, rows), :] = low
        for k in bands(r, n, rows, kept):
            hit = down == starts[0, vec + k : vec + k + 1, :] - rows * r
            affinity[k : k + 1, :] += jnp.sum(jnp.where(hit, dense, 0.0), axis=0, keepdims=True)

    score(0)
    for e in arrival_order:
        arrived(units, 1, e)
        forward_on(units, 1, e)
        score(e)
    for r in range(1, n, 2):
        arrived(units, 1, r)
        score(r)

    def product(wide):
        out = jnp.zeros((vec, rows), jnp.float32)
        step = min(total, 2048)
        for at in range(0, total, step):
            high, low = split(wide[:, at : at + step])
            cut = pl.ds(at, step)
            both = jnp.dot(
                jnp.concatenate([high, low], axis=0), s_high[cut, :],
                preferred_element_type=jnp.float32,
            )
            rest = jnp.dot(high, s_low[cut, :], preferred_element_type=jnp.float32)
            out = out + (both[:vec] + (both[vec:] + rest))
        return out

    def gram_of(wide):
        return lax.dot_general(
            wide, wide, (((1,), (1,)), ((), ())), precision=HIGH,
            preferred_element_type=jnp.float32,
        )

    mixed = product(jnp.concatenate([starts[r, :vec, :] for r in range(n)], axis=1))
    for turn in range(ITERS - 1):
        buffer, phase = mixes.at[turn], 2 + turn
        buffer[0] = mixed
        launch(buffer, phase)
        for e in arrival_order:
            arrived(buffer, phase, e)
            forward_on(buffer, phase, e)
        for r in range(1, n, 2):
            arrived(buffer, phase, r)
        wide = jnp.concatenate([buffer[r] for r in range(n)], axis=1)
        factor = inverse_factor(gram_of(wide))
        mixed = jnp.dot(factor, product(wide), precision=HIGH, preferred_element_type=jnp.float32)

    phase = ITERS + 1
    part = gram_of(mixed)
    pack = vec // 8
    packed = jnp.concatenate([part[8 * i : 8 * i + 8, :] for i in range(pack)], axis=1)
    grams[0] = packed
    for ahead in range(1, n):
        copy = remote(
            grams.at[0], grams.at[n - ahead], send_sem.at[phase, ahead],
            recv_sem.at[phase, n - ahead], lax.rem(me + ahead, n),
        )
        copy.start()
        sent.append(copy)
    for r in range(1, n):
        arrived(grams, phase, r)
        packed = packed + grams[r]
    gram = jnp.concatenate([packed[:, vec * i : vec * i + vec] for i in range(pack)], axis=0)
    factor = inverse_factor(gram)
    vectors[...] = jnp.dot(factor, mixed, precision=HIGH, preferred_element_type=jnp.float32)
    halo_copy.wait_send()
    for copy in sent:
        copy.wait_send()


def solution(mesh):
    n = mesh.shape["rows"]

    def on_device(frames, offsets, neighbours, initial_codes, embed_weight, embed_bias):
        own_frames, channels = frames.shape
        kept, rows = neighbours.shape
        vec = initial_codes.shape[0]
        width = embed_weight.shape[1]
        here = pl.BlockSpec(memory_space=pltpu.VMEM)
        there = pl.BlockSpec(memory_space=pl.ANY)
        phases = ITERS + 2
        return pl.pallas_call(
            functools.partial(kernel, n),
            out_shape=(
                jax.ShapeDtypeStruct((kept, rows), jnp.float32),
                jax.ShapeDtypeStruct((vec, rows), jnp.float32),
            ),
            in_specs=[there, there, here, here, here, here],
            out_specs=(here, here),
            scratch_shapes=[
                pltpu.VMEM((own_frames, channels), jnp.bfloat16),
                pltpu.VMEM((channels, width), jnp.bfloat16),
                pltpu.VMEM((HALO, channels), jnp.bfloat16),
                pltpu.VMEM((rows, channels), jnp.float32),
                pltpu.VMEM((n, rows, width), jnp.bfloat16),
                pltpu.VMEM((n, vec + kept, rows), jnp.float32),
                pltpu.VMEM((n, rows, rows), jnp.float32),
                pltpu.VMEM((n * rows, rows), jnp.bfloat16),
                pltpu.VMEM((n * rows, rows), jnp.bfloat16),
                pltpu.VMEM((ITERS - 1, n, vec, rows), jnp.float32),
                pltpu.VMEM((n, 8, vec * vec // 8), jnp.float32),
                pltpu.SemaphoreType.DMA((channels // 128 + 1,)),
                pltpu.SemaphoreType.DMA((2,)),
                pltpu.SemaphoreType.DMA((phases, n)),
                pltpu.SemaphoreType.DMA((phases, n)),
                pltpu.SemaphoreType.DMA((phases, n)),
            ],
            compiler_params=pltpu.CompilerParams(
                collective_id=0, has_side_effects=True, vmem_limit_bytes=60 * 1024 * 1024
            ),
        )(
            frames, embed_weight, offsets.reshape(1, rows), neighbours, initial_codes,
            embed_bias.reshape(1, width),
        )

    placed = (
        P(("groups", "rows"), None),
        P(("groups", "rows")),
        P(None, ("groups", "rows")),
        P(None, ("groups", "rows")),
        P(),
        P(),
    )
    return jax.shard_map(
        on_device,
        mesh=mesh,
        in_specs=placed,
        out_specs=(P(None, ("groups", "rows")), P(None, ("groups", "rows"))),
        check_vma=False,
    )
```

time: 475 us -> 62.9 us (0.13)
  waiting for transfers between devices: 131 us -> 0 us
  blocking collectives: 128 us -> 0 us
  other arithmetic: 105 us -> 0 us
  local copies, waits for them, and re-layouts: 81.2 us -> 2.65 us
  Pallas kernels: 0 us -> 59.1 us
  matrix products: 13.5 us -> 0 us
  between operations: 14 us -> 0.64 us
    reduce_scatter x3 -> x0, waiting for transfers between devices: 126 us -> none  [on_device(): lax.psum_scatter(spread, 'rows', scatter_dimension=1, tiled=True)]
    gather x6 -> x0, local copies, waits for them, and re-layouts: 75.2 us -> none  [the longest x3 42.3 us: on_device(): jnp.take(gathered, neighbours, axis=1)]
    all_gather x3 -> x0, blocking collectives: 70.3 us -> none  [on_device(): gathered = lax.all_gather(carried, 'rows', axis=1, tiled=True)]
    scatter-add x3 -> x0, other arithmetic: 70.2 us -> none  [on_device(): spread = jnp.zeros((vec_count, gathered.shape[1]), jnp.float32).at[:, nei...]
    pallas_call x0 -> x1, Pallas kernels: none -> 59.1 us  [on_device(): pl.pallas_call(functools.partial(kernel, n), out_shape=(jax.ShapeDtypeStr...]
    psum x1 -> x0, blocking collectives: 57.6 us -> none  [on_device(): gram_matrix = lax.psum(partial_gram, 'rows')]
    another operation x15 -> x0, other arithmetic: 20.1 us -> none  [the longest x9 10.8 us: on_device(): cholesky_factor = jnp.linalg.cholesky(gram_matrix)]
    reduce_sum x3 -> x0, other arithmetic: 9.57 us -> none  [on_device(): jnp.sum(affinity[None] * jnp.take(gathered, neighbours, axis=1), axis=1)]
  transfers between devices with their start and end apart: 5 -> 0, of which waited for: 5 -> 0; matrix products, arithmetic and copies ran while one was open for 12% -> 0% of each run, Pallas kernels for 0% -> 0%
where the time goes in v1:
time: 62.9 us; the launch traced here: 62.4 us
  Pallas kernels  59.1 us (94%)
  local copies, waits for them, and re-layouts  2.65 us (4%)
  between operations  0.64 us (1%)
    pallas_call x1, Pallas kernels, on_device(): pl.pallas_call(functools.partial(kernel, n), out_shape=(jax.ShapeDtypeStr...  59.1 us
    unnamed x2, local copies, waits for them, and re-layouts  2.65 us

profile of v1, /device:TPU:0, one launch (start us, length us, event | category | flops | bytes accessed | tf_op | source)
XLA Modules:
  0.0 62.4 jit_solution(7925427076003872391)
XLA Ops:
  0.6 59.1 %shard_map.77 = (f32[32,128]{1,0:T(8,128)}, f32[32,128]{1,0:T(8,128)}) custom-call(bf16[512,2560]{1,0:T(8,128)(2,1)} %frames.1, bf16[2560,256]{1,0:T(8,128)(2,1)} %weight.1, s32[1,128]{1,0:T(1,128)} %bitcast.3, s32[32,128]{1,0:T(8,128)} %neighbours.1, s32[32,128]{1,0:T(8,128)} %codes.1, f32[1,256]{1,0:T(1,128)} %bitcast.2), custom_call_target="tpu_custom_call" | custom-call | tf_op jit(solution)/shard_map/pallas_call | solution.py:281
  59.8 1.3 %copy.10 = f32[32,128]{1,0:T(8,128)} copy(f32[32,128]{1,0:T(8,128)} %get-tuple-element.4) | data formatting | bytes 32768
  61.1 1.3 %copy.11 = f32[32,128]{1,0:T(8,128)} copy(f32[32,128]{1,0:T(8,128)} %get-tuple-element.5) | data formatting | bytes 32768

commit v2 on v1

--- a/solution.py
+++ b/solution.py
@@ -40,11 +40,18 @@
     lane = lax.broadcasted_iota(jnp.int32, (size, size), 1)
     eye = jnp.where(row == lane, 1.0, 0.0).astype(jnp.float32)
     work = jnp.concatenate([gram, eye], axis=1)
-    tall = lax.broadcasted_iota(jnp.int32, (size, 1), 0)
-    for j in range(size):
-        pivot_row = work[j : j + 1, :]
-        factor = work[:, j : j + 1] * (1.0 / work[j : j + 1, j : j + 1])
-        work = work - jnp.where(tall > j, factor, 0.0) * pivot_row
+    tall = lax.broadcasted_iota(jnp.int32, work.shape, 0)
+    group = 4 if size % 4 == 0 else 1
+    for j in range(0, size, group):
+        cols = [jnp.broadcast_to(work[:, j + t : j + t + 1], work.shape) for t in range(group)]
+        lines = [work[j + t : j + t + 1, :] for t in range(group)]
+        for t in range(group):
+            factor = cols[t] * (1.0 / cols[t][j + t : j + t + 1, :])
+            factor = jnp.where(tall > j + t, factor, 0.0)
+            work = work - factor * lines[t]
+            for u in range(t + 1, group):
+                lines[u] = lines[u] - factor[j + u : j + u + 1, :] * lines[t]
+                cols[u] = cols[u] - factor * cols[t][j + u : j + u + 1, :]
     diagonal = jnp.sum(jnp.where(row == lane, work[:, :size], 0.0), axis=1, keepdims=True)
     return work[:, size:] * lax.rsqrt(diagonal)
 
@@ -230,19 +237,26 @@
             preferred_element_type=jnp.float32,
         )
 
+    def apply(factor, value):
+        return jnp.dot(factor, value, precision=HIGH, preferred_element_type=jnp.float32)
+
     mixed = product(jnp.concatenate([starts[r, :vec, :] for r in range(n)], axis=1))
+    pending = None
     for turn in range(ITERS - 1):
         buffer, phase = mixes.at[turn], 2 + turn
         buffer[0] = mixed
         launch(buffer, phase)
+        factor = None if pending is None else inverse_factor(gram_of(pending))
         for e in arrival_order:
             arrived(buffer, phase, e)
             forward_on(buffer, phase, e)
         for r in range(1, n, 2):
             arrived(buffer, phase, r)
-        wide = jnp.concatenate([buffer[r] for r in range(n)], axis=1)
-        factor = inverse_factor(gram_of(wide))
-        mixed = jnp.dot(factor, product(wide), precision=HIGH, preferred_element_type=jnp.float32)
+        pending = jnp.concatenate([buffer[r] for r in range(n)], axis=1)
+        if factor is not None:
+            pending = apply(factor, pending)
+        mixed = product(pending)
+    mixed = apply(inverse_factor(gram_of(pending)), mixed)
 
     phase = ITERS + 1
     part = gram_of(mixed)
@@ -261,7 +275,7 @@
         packed = packed + grams[r]
     gram = jnp.concatenate([packed[:, vec * i : vec * i + vec] for i in range(pack)], axis=0)
     factor = inverse_factor(gram)
-    vectors[...] = jnp.dot(factor, mixed, precision=HIGH, preferred_element_type=jnp.float32)
+    vectors[...] = apply(factor, mixed)
     halo_copy.wait_send()
     for copy in sent:
         copy.wait_send()

time: 62.9 us -> 59.2 us (0.941)
  Pallas kernels: 59.1 us -> 55.5 us
    pallas_call x1, Pallas kernels: 59.1 us -> 55.5 us  [on_device(): pl.pallas_call(functools.partial(kernel, n), out_shape=(jax.ShapeDtypeStr...]
where the time goes in v2:
time: 59.2 us; the launch traced here: 58.8 us
  Pallas kernels  55.5 us (94%)
  local copies, waits for them, and re-layouts  2.65 us (4%)
  between operations  0.64 us (1%)
    pallas_call x1, Pallas kernels, on_device(): pl.pallas_call(functools.partial(kernel, n), out_shape=(jax.ShapeDtypeStr...  55.5 us
    unnamed x2, local copies, waits for them, and re-layouts  2.65 us

profile of v2, /device:TPU:0, one launch (start us, length us, event | category | flops | bytes accessed | tf_op | source)
XLA Modules:
  0.0 58.8 jit_solution(16569677896317371449)
XLA Ops:
  0.6 55.5 %shard_map.77 = (f32[32,128]{1,0:T(8,128)}, f32[32,128]{1,0:T(8,128)}) custom-call(bf16[512,2560]{1,0:T(8,128)(2,1)} %frames.1, bf16[2560,256]{1,0:T(8,128)(2,1)} %weight.1, s32[1,128]{1,0:T(1,128)} %bitcast.3, s32[32,128]{1,0:T(8,128)} %neighbours.1, s32[32,128]{1,0:T(8,128)} %codes.1, f32[1,256]{1,0:T(1,128)} %bitcast.2), custom_call_target="tpu_custom_call" | custom-call | tf_op jit(solution)/shard_map/pallas_call | solution.py:295
  56.2 1.3 %copy.10 = f32[32,128]{1,0:T(8,128)} copy(f32[32,128]{1,0:T(8,128)} %get-tuple-element.4) | data formatting | bytes 32768
  57.5 1.3 %copy.11 = f32[32,128]{1,0:T(8,128)} copy(f32[32,128]{1,0:T(8,128)} %get-tuple-element.5) | data formatting | bytes 32768
